TPU v7x, 32 devices: a whole 2x2x4 slice. The times are simulated.
32 devices in a mesh: pod: 8 (over z, y), data: 4 (over x, core).
Axes of the slice: x: 2, y: 2, z: 4, core: 2. Of those that a mesh axis runs over, the one named last changes fastest.
Arguments:
- w_first: float32 [12, 512, 2048], replicated
- w_second: float32 [12, 2048, 512], replicated
- m_first: float32 [12, 512, 2048], replicated
- m_second: float32 [12, 2048, 512], replicated
- x_now: bfloat16 [16384, 512], P(('pod', 'data'))
- y_now: bfloat16 [16384, 512], P(('pod', 'data'))
- x_next: bfloat16 [16384, 512], P(('pod', 'data'))
- y_next: bfloat16 [16384, 512], P(('pod', 'data'))
Outputs:
- output 1: float32 [12, 512, 2048], replicated
- output 2: float32 [12, 2048, 512], replicated
- output 3: float32 [12, 512, 2048], replicated
- output 4: float32 [12, 2048, 512], replicated
- output 5: float32 [16384], P(('pod', 'data'))
- output 6: float32 [16384, 512], P(('pod', 'data'))
All inputs are finite; a program needn't handle non-finite values.
Results may differ from a plain program's by a relative error of at most 0.0107373.
Values are sent between devices in bfloat16 or wider.
A program may use at most 1.75 GiB of HBM per device.

v0:
```python
import jax
import jax.numpy as jnp
from jax import lax
from jax.sharding import PartitionSpec as P

LEARN_BASE = 0.25
MOMENTUM = 0.9


def solution(mesh):
    n_pod = mesh.shape['pod']
    n_data = mesh.shape['data']
    rows_spec = P(('pod', 'data'), None)
    full_spec = P()

    def reduce_grad(grad_low, scatter_dim):
        shard_sum = lax.psum_scatter(grad_low, 'data', scatter_dimension=scatter_dim, tiled=True)
        shard_sum = lax.psum(shard_sum, 'pod')
        return lax.all_gather(shard_sum, 'data', axis=scatter_dim, tiled=True).astype(jnp.float32)

    def train_step(w_first, w_second, m_first, m_second, x_now, y_now, x_next, y_next):
        layers = w_first.shape[0]
        model_width = w_first.shape[1]
        batch_total = x_now.shape[0] * n_pod * n_data
        learn_rate = LEARN_BASE / layers
        wf_low = w_first.astype(jnp.bfloat16)
        ws_low = w_second.astype(jnp.bfloat16)
        hidden = x_now.astype(jnp.float32)
        saved_acts = []
        for layer_idx in range(layers):
            h_low = hidden.astype(jnp.bfloat16)
            pre_act = jnp.dot(h_low, wf_low[layer_idx], preferred_element_type=jnp.float32)
            act_val, gelu_back = jax.vjp(jax.nn.gelu, pre_act)
            act_low = act_val.astype(jnp.bfloat16)
            hidden = hidden + jnp.dot(act_low, ws_low[layer_idx], preferred_element_type=jnp.float32)
            saved_acts.append((h_low, act_low, gelu_back))
        grad_h = (hidden - y_now.astype(jnp.float32)) / (batch_total * model_width)
        sum_first = [None] * layers
        sum_second = [None] * layers
        for layer_idx in reversed(range(layers)):
            h_low, act_low, gelu_back = saved_acts[layer_idx]
            grad_low = grad_h.astype(jnp.bfloat16)
            g_second = jnp.einsum('bf,bd->fd', act_low, grad_low, preferred_element_type=jnp.float32)
            grad_act = jnp.einsum('bd,fd->bf', grad_low, ws_low[layer_idx], preferred_element_type=jnp.float32)
            grad_pre = gelu_back(grad_act)[0].astype(jnp.bfloat16)
            g_first = jnp.einsum('bd,bf->df', h_low, grad_pre, preferred_element_type=jnp.float32)
            if layer_idx > 0:
                grad_h = grad_h + jnp.einsum('bf,df->bd', grad_pre, wf_low[layer_idx], preferred_element_type=jnp.float32)
            sum_second[layer_idx] = reduce_grad(g_second.astype(jnp.bfloat16), 0)
            sum_first[layer_idx] = reduce_grad(g_first.astype(jnp.bfloat16), 1)
        new_wf, new_ws, new_mf, new_ms = [], [], [], []
        hidden = x_next.astype(jnp.float32)
        for layer_idx in range(layers):
            mom_first = MOMENTUM * m_first[layer_idx] + sum_first[layer_idx]
            mom_second = MOMENTUM * m_second[layer_idx] + sum_second[layer_idx]
            weight_first = w_first[layer_idx] - learn_rate * mom_first
            weight_second = w_second[layer_idx] - learn_rate * mom_second
            new_mf.append(mom_first)
            new_ms.append(mom_second)
            new_wf.append(weight_first)
            new_ws.append(weight_second)
            pre_act = jnp.dot(hidden.astype(jnp.bfloat16), weight_first.astype(jnp.bfloat16), preferred_element_type=jnp.float32)
            act_low = jax.nn.gelu(pre_act).astype(jnp.bfloat16)
            hidden = hidden + jnp.dot(act_low, weight_second.astype(jnp.bfloat16), preferred_element_type=jnp.float32)
        resid_rows = hidden - y_next.astype(jnp.float32)
        loss_rows = jnp.sum(resid_rows * resid_rows, axis=-1) / (2 * model_width)
        return (jnp.stack(new_wf), jnp.stack(new_ws), jnp.stack(new_mf), jnp.stack(new_ms), loss_rows, hidden)

    return jax.shard_map(train_step, mesh=mesh,
                         in_specs=(full_spec,) * 4 + (rows_spec,) * 4,
                         out_specs=(full_spec,) * 4 + (P(('pod', 'data')), rows_spec),
                         check_vma=False)
```

profile of v0, /device:TPU:0, one launch (start us, length us, event | category | flops | bytes accessed | tf_op | source)
XLA Modules:
  0.0 2272.1 jit_solution(15468849595871919522)
XLA Ops:
  7.2 25.6 %convert_element_type.452 = bf16[12,2048,512]{2,1,0:T(8,128)(2,1)} convert(f32[12,2048,512]{2,1,0:T(8,128)} %param.9) | non-fusion elementwise | flops 12582912 | bytes 75497472 | tf_op jit(solution)/shard_map/convert_element_type | solution.py:27
  32.9 25.9 %convert_element_type.450 = bf16[12,512,2048]{2,1,0:T(8,128)(2,1)} convert(f32[12,512,2048]{2,1,0:T(8,128)} %param.8) | non-fusion elementwise | flops 12582912 | bytes 75497472 | tf_op jit(solution)/shard_map/convert_element_type | solution.py:26
  346.2 33.6 %reduce-scatter.41.cloned.1.call-done = bf16[512,512]{0,1:T(8,128)(2,1)} async-done(((bf16[512,2048]{0,1:T(8,128)(2,1)}), bf16[512,512]{0,1:T(8,128)(2,1)}) %reduce-scatter.41.cloned.1.call-update) | async-done | bytes 524304 | tf_op jit(solution)/shard_map/reduce_scatter | solution.py:17
  379.9 33.6 %reduce-scatter.65.cloned.1.call-done = bf16[512,512]{1,0:T(8,128)(2,1)} async-done(((bf16[2048,512]{1,0:T(8,128)(2,1)}), bf16[512,512]{1,0:T(8,128)(2,1)}) %reduce-scatter.65.cloned.1.call-update) | async-done | bytes 524304 | tf_op jit(solution)/shard_map/reduce_scatter | solution.py:17
  413.5 33.6 %reduce-scatter.39.cloned.1.call-done = bf16[512,512]{0,1:T(8,128)(2,1)} async-done(((bf16[512,2048]{0,1:T(8,128)(2,1)}), bf16[512,512]{0,1:T(8,128)(2,1)}) %reduce-scatter.39.cloned.1.call-update) | async-done | bytes 524304 | tf_op jit(solution)/shard_map/reduce_scatter | solution.py:17
  447.1 33.5 %reduce-scatter.63.cloned.1.call-done = bf16[512,512]{1,0:T(8,128)(2,1)} async-done(((bf16[2048,512]{1,0:T(8,128)(2,1)}), bf16[512,512]{1,0:T(8,128)(2,1)}) %reduce-scatter.63.cloned.1.call-update) | async-done | bytes 524304 | tf_op jit(solution)/shard_map/reduce_scatter | solution.py:17
  480.6 33.6 %reduce-scatter.37.cloned.1.call-done = bf16[512,512]{0,1:T(8,128)(2,1)} async-done(((bf16[512,2048]{0,1:T(8,128)(2,1)}), bf16[512,512]{0,1:T(8,128)(2,1)}) %reduce-scatter.37.cloned.1.call-update) | async-done | bytes 524304 | tf_op jit(solution)/shard_map/reduce_scatter | solution.py:17
  514.2 33.5 %reduce-scatter.61.cloned.1.call-done = bf16[512,512]{1,0:T(8,128)(2,1)} async-done(((bf16[2048,512]{1,0:T(8,128)(2,1)}), bf16[512,512]{1,0:T(8,128)(2,1)}) %reduce-scatter.61.cloned.1.call-update) | async-done | bytes 524304 | tf_op jit(solution)/shard_map/reduce_scatter | solution.py:17
  547.7 33.6 %reduce-scatter.35.cloned.1.call-done = bf16[512,512]{0,1:T(8,128)(2,1)} async-done(((bf16[512,2048]{0,1:T(8,128)(2,1)}), bf16[512,512]{0,1:T(8,128)(2,1)}) %reduce-scatter.35.cloned.1.call-update) | async-done | bytes 524304 | tf_op jit(solution)/shard_map/reduce_scatter | solution.py:17
  581.3 33.5 %reduce-scatter.59.cloned.1.call-done = bf16[512,512]{1,0:T(8,128)(2,1)} async-done(((bf16[2048,512]{1,0:T(8,128)(2,1)}), bf16[512,512]{1,0:T(8,128)(2,1)}) %reduce-scatter.59.cloned.1.call-update) | async-done | bytes 524304 | tf_op jit(solution)/shard_map/reduce_scatter | solution.py:17
  614.8 33.5 %reduce-scatter.33.cloned.1.call-done = bf16[512,512]{0,1:T(8,128)(2,1)} async-done(((bf16[512,2048]{0,1:T(8,128)(2,1)}), bf16[512,512]{0,1:T(8,128)(2,1)}) %reduce-scatter.33.cloned.1.call-update) | async-done | bytes 524304 | tf_op jit(solution)/shard_map/reduce_scatter | solution.py:17
  648.3 33.5 %reduce-scatter.57.cloned.1.call-done = bf16[512,512]{1,0:T(8,128)(2,1)} async-done(((bf16[2048,512]{1,0:T(8,128)(2,1)}), bf16[512,512]{1,0:T(8,128)(2,1)}) %reduce-scatter.57.cloned.1.call-update) | async-done | bytes 524304 | tf_op jit(solution)/shard_map/reduce_scatter | solution.py:17
  681.8 33.5 %reduce-scatter.31.cloned.1.call-done = bf16[512,512]{0,1:T(8,128)(2,1)} async-done(((bf16[512,2048]{0,1:T(8,128)(2,1)}), bf16[512,512]{0,1:T(8,128)(2,1)}) %reduce-scatter.31.cloned.1.call-update) | async-done | bytes 524304 | tf_op jit(solution)/shard_map/reduce_scatter | solution.py:17
  715.3 33.5 %reduce-scatter.55.cloned.1.call-done = bf16[512,512]{1,0:T(8,128)(2,1)} async-done(((bf16[2048,512]{1,0:T(8,128)(2,1)}), bf16[512,512]{1,0:T(8,128)(2,1)}) %reduce-scatter.55.cloned.1.call-update) | async-done | bytes 524304 | tf_op jit(solution)/shard_map/reduce_scatter | solution.py:17
  748.7 33.6 %reduce-scatter.29.cloned.1.call-done = bf16[512,512]{0,1:T(8,128)(2,1)} async-done(((bf16[512,2048]{0,1:T(8,128)(2,1)}), bf16[512,512]{0,1:T(8,128)(2,1)}) %reduce-scatter.29.cloned.1.call-update) | async-done | bytes 524304 | tf_op jit(solution)/shard_map/reduce_scatter | solution.py:17
  782.4 33.5 %reduce-scatter.53.cloned.1.call-done = bf16[512,512]{1,0:T(8,128)(2,1)} async-done(((bf16[2048,512]{1,0:T(8,128)(2,1)}), bf16[512,512]{1,0:T(8,128)(2,1)}) %reduce-scatter.53.cloned.1.call-update) | async-done | bytes 524304 | tf_op jit(solution)/shard_map/reduce_scatter | solution.py:17
  815.8 34.2 %reduce-scatter.27.cloned.1.call-done = bf16[512,512]{0,1:T(8,128)(2,1)} async-done(((bf16[512,2048]{0,1:T(8,128)(2,1)}), bf16[512,512]{0,1:T(8,128)(2,1)}) %reduce-scatter.27.cloned.1.call-update) | async-done | bytes 524304 | tf_op jit(solution)/shard_map/reduce_scatter | solution.py:17
  850.0 33.6 %reduce-scatter.49.cloned.1.call-done = bf16[512,512]{1,0:T(8,128)(2,1)} async-done(((bf16[2048,512]{1,0:T(8,128)(2,1)}), bf16[512,512]{1,0:T(8,128)(2,1)}) %reduce-scatter.49.cloned.1.call-update) | async-done | bytes 524304 | tf_op jit(solution)/shard_map/reduce_scatter | solution.py:17
  883.7 33.6 %reduce-scatter.51.cloned.1.call-done = bf16[512,512]{1,0:T(8,128)(2,1)} async-done(((bf16[2048,512]{1,0:T(8,128)(2,1)}), bf16[512,512]{1,0:T(8,128)(2,1)}) %reduce-scatter.51.cloned.1.call-update) | async-done | bytes 524304 | tf_op jit(solution)/shard_map/reduce_scatter | solution.py:17
  917.3 34.1 %reduce-scatter.25.cloned.1.call-done = bf16[512,512]{0,1:T(8,128)(2,1)} async-done(((bf16[512,2048]{0,1:T(8,128)(2,1)}), bf16[512,512]{0,1:T(8,128)(2,1)}) %reduce-scatter.25.cloned.1.call-update) | async-done | bytes 524304 | tf_op jit(solution)/shard_map/reduce_scatter | solution.py:17
  951.4 446.5 %all-reduce.3.cloned.1.call-done = (bf16[512,512]{0,1:T(8,128)(2,1)}, bf16[512,512]{0,1:T(8,128)(2,1)}, bf16[512,512]{0,1:T(8,128)(2,1)}, bf16[512,512]{0,1:T(8,...) async-done(((bf16[512,512]{0,1:T(8,128)(2,1)}, ...) | async-done | bytes 12582928 | tf_op jit(solution)/shard_map/psum | solution.py:18
  1413.3 33.0 %fusion.553 = (f32[1,512,2048]{2,1,0:T(8,128)}, f32[1,512,2048]{2,1,0:T(8,128)}, f32[1,512,2048]{2,1,0:T(8,128)}, f32[1,512,2048]{2,1,0:T(8,128)}, f32[1,512,204...) fusion(f32[12,512,2048]{2,1,0:T(8,128)} %param.10), kind=kLoop, calls=%fused_computation.641 | loop fusion | bytes 100663296 | tf_op jit(solution)/shard_map/slice | solution.py:54
  1510.6 33.0 %fusion.552 = (f32[1,512,2048]{2,1,0:T(8,128)}, f32[1,512,2048]{2,1,0:T(8,128)}, f32[1,512,2048]{2,1,0:T(8,128)}, f32[1,512,2048]{2,1,0:T(8,128)}, f32[1,512,204...) fusion(f32[12,512,2048]{2,1,0:T(8,128)} %param.8), kind=kLoop, calls=%fused_computation.640 | loop fusion | bytes 100663296 | tf_op jit(solution)/shard_map/slice | solution.py:56
  1661.6 23.0 %all-gather.59.cloned.1.call-done = bf16[2048,512]{1,0:T(8,128)(2,1)} async-done(((bf16[512,512]{1,0:T(8,128)(2,1)}), bf16[2048,512]{1,0:T(8,128)(2,1)}) %all-gather.59.cloned.1.call-update) | async-done | bytes 2097168 | tf_op jit(solution)/shard_map/all_gather | solution.py:19
  1708.6 23.8 %all-gather.61.cloned.1.call-done = bf16[2048,512]{1,0:T(8,128)(2,1)} async-done(((bf16[512,512]{1,0:T(8,128)(2,1)}), bf16[2048,512]{1,0:T(8,128)(2,1)}) %all-gather.61.cloned.1.call-update) | async-done | bytes 2097168 | tf_op jit(solution)/shard_map/all_gather | solution.py:19
  1756.3 23.9 %all-gather.63.cloned.1.call-done = bf16[2048,512]{1,0:T(8,128)(2,1)} async-done(((bf16[512,512]{1,0:T(8,128)(2,1)}), bf16[2048,512]{1,0:T(8,128)(2,1)}) %all-gather.63.cloned.1.call-update) | async-done | bytes 2097168 | tf_op jit(solution)/shard_map/all_gather | solution.py:19
  1804.1 23.8 %all-gather.65.cloned.1.call-done = bf16[2048,512]{1,0:T(8,128)(2,1)} async-done(((bf16[512,512]{1,0:T(8,128)(2,1)}), bf16[2048,512]{1,0:T(8,128)(2,1)}) %all-gather.65.cloned.1.call-update) | async-done | bytes 2097168 | tf_op jit(solution)/shard_map/all_gather | solution.py:19
  1851.7 23.8 %all-gather.67.cloned.1.call-done = bf16[2048,512]{1,0:T(8,128)(2,1)} async-done(((bf16[512,512]{1,0:T(8,128)(2,1)}), bf16[2048,512]{1,0:T(8,128)(2,1)}) %all-gather.67.cloned.1.call-update) | async-done | bytes 2097168 | tf_op jit(solution)/shard_map/all_gather | solution.py:19
  1899.3 23.8 %all-gather.69.cloned.1.call-done = bf16[2048,512]{1,0:T(8,128)(2,1)} async-done(((bf16[512,512]{1,0:T(8,128)(2,1)}), bf16[2048,512]{1,0:T(8,128)(2,1)}) %all-gather.69.cloned.1.call-update) | async-done | bytes 2097168 | tf_op jit(solution)/shard_map/all_gather | solution.py:19
  1946.8 23.8 %all-gather.71.cloned.1.call-done = bf16[2048,512]{1,0:T(8,128)(2,1)} async-done(((bf16[512,512]{1,0:T(8,128)(2,1)}), bf16[2048,512]{1,0:T(8,128)(2,1)}) %all-gather.71.cloned.1.call-update) | async-done | bytes 2097168 | tf_op jit(solution)/shard_map/all_gather | solution.py:19
  2062.3 49.5 %copy.53 = f32[12,512,2048]{2,1,0:T(8,128)} copy(f32[12,512,2048]{1,2,0:T(8,128)} %get-tuple-element.84) | data formatting | bytes 100663296
  2111.8 49.8 %copy.52 = f32[12,512,2048]{2,1,0:T(8,128)} copy(f32[12,512,2048]{1,2,0:T(8,128)} %get-tuple-element.85) | data formatting | bytes 100663296
  (467 shorter events, 821.0 us)
Async XLA Ops:
  7.2 338.9 %reduce-scatter.47.cloned.1.call-start = ((), (), s32[]{:S(2)}) async-start(), calls=%async_computation.46 | async-start | bytes 2621440 | tf_op jit(solution)/shard_map/reduce_scatter | solution.py:17
  221.8 258.8 %reduce-scatter.63.cloned.1.call-start = ((), (), s32[]{:S(2)}) async-start(), calls=%async_computation.62 | async-start | bytes 2621440 | tf_op jit(solution)/shard_map/reduce_scatter | solution.py:17
  227.7 286.5 %reduce-scatter.37.cloned.1.call-start = ((), (), s32[]{:S(2)}) async-start(), calls=%async_computation.36 | async-start | bytes 2621440 | tf_op jit(solution)/shard_map/reduce_scatter | solution.py:17
  239.4 308.3 %reduce-scatter.61.cloned.1.call-start = ((), (), s32[]{:S(2)}) async-start(), calls=%async_computation.60 | async-start | bytes 2621440 | tf_op jit(solution)/shard_map/reduce_scatter | solution.py:17
  245.2 336.1 %reduce-scatter.35.cloned.1.call-start = ((), (), s32[]{:S(2)}) async-start(), calls=%async_computation.34 | async-start | bytes 2621440 | tf_op jit(solution)/shard_map/reduce_scatter | solution.py:17
  256.6 358.2 %reduce-scatter.59.cloned.1.call-start = ((), (), s32[]{:S(2)}) async-start(), calls=%async_computation.58 | async-start | bytes 2621440 | tf_op jit(solution)/shard_map/reduce_scatter | solution.py:17
  262.5 385.8 %reduce-scatter.33.cloned.1.call-start = ((), (), s32[]{:S(2)}) async-start(), calls=%async_computation.32 | async-start | bytes 2621440 | tf_op jit(solution)/shard_map/reduce_scatter | solution.py:17
  274.1 407.7 %reduce-scatter.57.cloned.1.call-start = ((), (), s32[]{:S(2)}) async-start(), calls=%async_computation.56 | async-start | bytes 2621440 | tf_op jit(solution)/shard_map/reduce_scatter | solution.py:17
  280.0 435.2 %reduce-scatter.31.cloned.1.call-start = ((), (), s32[]{:S(2)}) async-start(), calls=%async_computation.30 | async-start | bytes 2621440 | tf_op jit(solution)/shard_map/reduce_scatter | solution.py:17
  291.3 457.4 %reduce-scatter.55.cloned.1.call-start = ((), (), s32[]{:S(2)}) async-start(), calls=%async_computation.54 | async-start | bytes 2621440 | tf_op jit(solution)/shard_map/reduce_scatter | solution.py:17
  297.2 485.2 %reduce-scatter.29.cloned.1.call-start = ((), (), s32[]{:S(2)}) async-start(), calls=%async_computation.28 | async-start | bytes 2621440 | tf_op jit(solution)/shard_map/reduce_scatter | solution.py:17
  308.9 507.0 %reduce-scatter.53.cloned.1.call-start = ((), (), s32[]{:S(2)}) async-start(), calls=%async_computation.52 | async-start | bytes 2621440 | tf_op jit(solution)/shard_map/reduce_scatter | solution.py:17
  314.6 535.4 %reduce-scatter.27.cloned.1.call-start = ((), (), s32[]{:S(2)}) async-start(), calls=%async_computation.26 | async-start | bytes 2621440 | tf_op jit(solution)/shard_map/reduce_scatter | solution.py:17
  325.9 557.8 %reduce-scatter.49.cloned.1.call-start = ((), (), s32[]{:S(2)}) async-start(), calls=%async_computation.48 | async-start | bytes 2621440 | tf_op jit(solution)/shard_map/reduce_scatter | solution.py:17
  333.1 584.2 %reduce-scatter.51.cloned.1.call-start = ((), (), s32[]{:S(2)}) async-start(), calls=%async_computation.50 | async-start | bytes 2621440 | tf_op jit(solution)/shard_map/reduce_scatter | solution.py:17
  338.8 612.6 %reduce-scatter.25.cloned.1.call-start = ((), (), s32[]{:S(2)}) async-start(), calls=%async_computation.24 | async-start | bytes 2621440 | tf_op jit(solution)/shard_map/reduce_scatter | solution.py:17
  346.0 1051.9 %all-reduce.3.cloned.1.call-start = ((), (), s32[]{:S(2)}) async-start(), calls=%async_computation.72 | async-start | bytes 25165824 | tf_op jit(solution)/shard_map/psum | solution.py:18
  951.4 656.9 %all-gather.25.cloned.1.call-start = ((), (), s32[]{:S(2)}) async-start(), calls=%async_computation.25 | async-start | bytes 2621440 | tf_op jit(solution)/shard_map/all_gather | solution.py:19
  1404.1 257.5 %all-gather.35.cloned.1.call-start = ((), (), s32[]{:S(2)}) async-start(), calls=%async_computation.35 | async-start | bytes 2621440 | tf_op jit(solution)/shard_map/all_gather | solution.py:19
  1404.7 279.9 %all-gather.59.cloned.1.call-start = ((), (), s32[]{:S(2)}) async-start(), calls=%async_computation.59 | async-start | bytes 2621440 | tf_op jit(solution)/shard_map/all_gather | solution.py:19
  1405.3 303.3 %all-gather.37.cloned.1.call-start = ((), (), s32[]{:S(2)}) async-start(), calls=%async_computation.37 | async-start | bytes 2621440 | tf_op jit(solution)/shard_map/all_gather | solution.py:19
  1406.1 326.3 %all-gather.61.cloned.1.call-start = ((), (), s32[]{:S(2)}) async-start(), calls=%async_computation.61 | async-start | bytes 2621440 | tf_op jit(solution)/shard_map/all_gather | solution.py:19
  1406.6 349.6 %all-gather.39.cloned.1.call-start = ((), (), s32[]{:S(2)}) async-start(), calls=%async_computation.39 | async-start | bytes 2621440 | tf_op jit(solution)/shard_map/all_gather | solution.py:19
  1407.4 372.8 %all-gather.63.cloned.1.call-start = ((), (), s32[]{:S(2)}) async-start(), calls=%async_computation.63 | async-start | bytes 2621440 | tf_op jit(solution)/shard_map/all_gather | solution.py:19
  1408.1 396.0 %all-gather.41.cloned.1.call-start = ((), (), s32[]{:S(2)}) async-start(), calls=%async_computation.41 | async-start | bytes 2621440 | tf_op jit(solution)/shard_map/all_gather | solution.py:19
  1408.8 419.0 %all-gather.65.cloned.1.call-start = ((), (), s32[]{:S(2)}) async-start(), calls=%async_computation.65 | async-start | bytes 2621440 | tf_op jit(solution)/shard_map/all_gather | solution.py:19
  1409.4 442.3 %all-gather.43.cloned.1.call-start = ((), (), s32[]{:S(2)}) async-start(), calls=%async_computation.43 | async-start | bytes 2621440 | tf_op jit(solution)/shard_map/all_gather | solution.py:19
  1410.2 465.3 %all-gather.67.cloned.1.call-start = ((), (), s32[]{:S(2)}) async-start(), calls=%async_computation.67 | async-start | bytes 2621440 | tf_op jit(solution)/shard_map/all_gather | solution.py:19
  1410.8 488.5 %all-gather.45.cloned.1.call-start = ((), (), s32[]{:S(2)}) async-start(), calls=%async_computation.45 | async-start | bytes 2621440 | tf_op jit(solution)/shard_map/all_gather | solution.py:19
  1411.3 511.7 %all-gather.69.cloned.1.call-start = ((), (), s32[]{:S(2)}) async-start(), calls=%async_computation.69 | async-start | bytes 2621440 | tf_op jit(solution)/shard_map/all_gather | solution.py:19
  1411.9 534.9 %all-gather.47.cloned.1.call-start = ((), (), s32[]{:S(2)}) async-start(), calls=%async_computation.47 | async-start | bytes 2621440 | tf_op jit(solution)/shard_map/all_gather | solution.py:19
  1413.3 557.3 %all-gather.71.cloned.1.call-start = ((), (), s32[]{:S(2)}) async-start(), calls=%async_computation.71 | async-start | bytes 2621440 | tf_op jit(solution)/shard_map/all_gather | solution.py:19
  (123 other events, 4318.0 us)
Sparse Core Ops, SparseCore 0:
  144.7 33.8 reduce-scatter.46
  181.1 31.0 reduce-scatter.70
  214.7 31.0 reduce-scatter.44
  248.2 31.0 reduce-scatter.68
  281.7 31.0 reduce-scatter.42
  315.1 31.0 reduce-scatter.66
  348.8 31.0 reduce-scatter.40
  382.4 31.0 reduce-scatter.64
  416.0 31.0 reduce-scatter.38
  449.5 31.0 reduce-scatter.62
  483.1 31.0 reduce-scatter.36
  516.6 31.0 reduce-scatter.60
  550.2 31.0 reduce-scatter.34
  583.7 31.0 reduce-scatter.58
  617.2 31.0 reduce-scatter.32
  650.7 31.0 reduce-scatter.56
  684.2 31.0 reduce-scatter.30
  717.6 31.0 reduce-scatter.54
  751.3 31.0 reduce-scatter.28
  784.7 31.0 reduce-scatter.52
  818.9 31.0 reduce-scatter.26
  852.6 31.0 reduce-scatter.48
  886.2 31.0 reduce-scatter.50
  920.3 31.0 reduce-scatter.24
  957.8 440.0 all-reduce.2
  1447.7 22.3 all-gather.26
  1471.6 22.3 all-gather.50
  1495.4 22.3 all-gather.28
  1543.2 22.3 all-gather.30
  1567.0 22.3 all-gather.54
  1686.2 22.3 all-gather.36
  1710.0 22.3 all-gather.60
  (17 shorter events, 376.9 us)
where the time goes:
time: 2280 us; the launch traced here: 2270 us
  waiting for transfers between devices  1310 us (57%)
  matrix products  402 us (18%)
  local copies, waits for them, and re-layouts  312 us (14%)
  other arithmetic  229 us (10%)
    reduce_scatter x24, waiting for transfers between devices, reduce_grad(): lax.psum_scatter(grad_low, 'data', scatter_dimension=scatter_dim, tiled=T...  605 us
    psum x1, waiting for transfers between devices, reduce_grad(): shard_sum = lax.psum(shard_sum, 'pod')  446 us
    unnamed x241, local copies, waits for them, and re-layouts  247 us
    all_gather x24, waiting for transfers between devices, reduce_grad(): lax.all_gather(shard_sum, 'data', axis=scatter_dim, tiled=True)  244 us
    unnamed x22, other arithmetic  162 us
    dot_general x12, matrix products, train_step(): jnp.dot(act_low, weight_second.astype(jnp.bfloat16), preferred_element_ty...  130 us
    dot_general x12, matrix products, train_step(): jnp.einsum('bf,bd->fd', act_low, grad_low, preferred_element_type=jnp.flo...  66.3 us
    dot_general x11, matrix products, train_step(): jnp.einsum('bd,fd->bf', grad_low, ws_low[layer_idx], preferred_element_ty...  60.9 us
  transfers between devices with their start and end apart: 49, of which 32 were waited for; matrix products, arithmetic and copies ran while one was open for 22% of the time, Pallas kernels for 0%

commit v1 on v0

v1 whole, which is shorter than its diff:
```python
import functools

import jax
import jax.numpy as jnp
from jax import lax
from jax.experimental import pallas as pl
from jax.experimental.pallas import tpu as pltpu
from jax.sharding import PartitionSpec as P

MESH = pl.DeviceIdType.MESH
LEARN_BASE = 0.25
MOMENTUM = 0.9
GELU_C = 0.7978845608028654
GELU_A = 0.044715
BF, F32 = jnp.bfloat16, jnp.float32

L, D, F, R = 12, 512, 2048, 512
FT = 256
TPL = F // FT
NC = L * TPL
NT = NC // 3
PR = 64
RING = 48
SLOTS, LAG, DEPTH = 4, 2, 13

CORE, DONE, OA, OB, OC, NTYPE = 0, 1, 2, 10, 18, 26
X, Y, ZU, ZD, GZU, GZD, GY, GX = range(8)
SLOT_PARTS = {}
for _base, _order in ((OA, "xyz"), (OB, "yzx"), (OC, "zxy")):
    for _n, _ax in zip((4, 2, 1), _order):
        for _ty in {"x": (X,), "y": (Y,), "z": (ZU, ZD)}[_ax]:
            SLOT_PARTS[_base + _ty] = _n


def gelu(a):
    return 0.5 * a * (1.0 + jnp.tanh(GELU_C * (a + GELU_A * (a * a * a))))


def gelu_both(a):
    sq = a * a
    th = jnp.tanh(GELU_C * (a + GELU_A * (sq * a)))
    half = 0.5 * (1.0 + th)
    slope = half + 0.5 * a * (1.0 - th * th) * (GELU_C * (1.0 + 3.0 * GELU_A * sq))
    return a * half, slope


def dot(a, b, da=1, db=0):
    return lax.dot_general(a, b, (((da,), (db,)), ((), ())), preferred_element_type=F32)


class Net:
    def __init__(self, part, out, slots, ssem, rsem, csem, ksem):
        self.part, self.out, self.slots = part, out, slots
        self.ssem, self.rsem, self.csem, self.ksem = ssem, rsem, csem, ksem
        pod, data = lax.axis_index("pod"), lax.axis_index("data")
        z, y, x, core = pod // 2, lax.rem(pod, 2), data // 2, lax.rem(data, 2)
        self.z, self.y, self.x, self.core = z, y, x, core
        dev = lambda z, y, x, core: (z * 2 + y, x * 2 + core)
        self.xn, self.yn, self.cn = dev(z, y, 1 - x, core), dev(z, 1 - y, x, core), dev(z, y, x, 1 - core)
        self.up, self.dn = dev(z + 1, y, x, core), dev(z - 1, y, x, core)
        self.has_up, self.has_dn = z < 3, z > 0
        self.end, self.d = (z == 0) | (z == 3), z // 3

    def neighbours(self):
        return ((self.xn, None), (self.yn, None), (self.cn, None), (self.up, self.has_up), (self.dn, self.has_dn))

    def each(self, fn):
        for i, (n, cond) in enumerate(self.neighbours()):
            go = functools.partial(fn, i, n)
            if cond is None:
                go()
            else:
                pl.when(cond)(go)

    def barrier(self):
        sem = pltpu.get_barrier_semaphore()
        self.each(lambda i, n: pl.semaphore_signal(sem, inc=1, device_id=n, device_id_type=MESH))
        pl.semaphore_wait(sem, 3 + jnp.where(self.has_up, 1, 0) + jnp.where(self.has_dn, 1, 0))

    def give_credit(self):
        file = (0, 1, 2, 4, 3)
        self.each(lambda i, n: pl.semaphore_signal(self.csem.at[file[i]], inc=1, device_id=n, device_id_type=MESH))

    def take_credit(self):
        self.each(lambda i, n: pl.semaphore_wait(self.csem.at[i], 1))

    def ok(self, t, cond=None):
        valid = (t >= 0) & (t < NT)
        return valid if cond is None else valid & cond

    def copy(self, ty, t, src, dst, to):
        s = lax.rem(t, SLOTS)
        return pltpu.make_async_remote_copy(src_ref=src, dst_ref=dst, send_sem=self.ssem.at[ty, s], recv_sem=self.rsem.at[ty, s],
                                            device_id=to, device_id_type=MESH)

    def slot(self, ty, t):
        return self.slots[ty].at[lax.rem(t, SLOTS)]

    def mine(self, c, first, n):
        return self.part.at[lax.rem(c, RING), pl.ds(first, n)]

    def full(self, c, first, n):
        return self.out.at[self.core, c, pl.ds(first, n)]

    def send(self, ty, t, cond, src, dst, to, like):
        pl.when(self.ok(t - 1, cond))(lambda: self.copy(ty, t - 1, like, like, to).wait_send())
        pl.when(self.ok(t, cond))(lambda: self.copy(ty, t, src, dst, to).start())

    def add(self, ty, t, cond, c, first, n, frm):
        def go():
            got = self.slot(ty, t)
            self.copy(ty, t, got, got, frm).wait_recv()
            row = lax.rem(c, RING)
            self.part[row, pl.ds(first, n)] = self.part[row, pl.ds(first, n)] + got[...]
        pl.when(self.ok(t, cond))(go)

    def pass_on(self, ty, t, cond, c, first, n, to):
        self.send(ty, t, cond, self.mine(c, first, n), self.slot(ty, t), to, self.mine(0, 0, n))

    def got(self, ty, t, cond, c, first, n, frm):
        ref = self.full(c, first, n)
        pl.when(self.ok(t, cond))(lambda: self.copy(ty, t, ref, ref, frm).wait_recv())

    def spread(self, ty, t, cond, c, first, n, to):
        self.send(ty, t, cond, self.full(c, first, n), self.full(c, first, n), to, self.mine(0, 0, n))

    def spread_own(self, ty, t, cond, c, first, n, to):
        self.send(ty, t, cond, self.mine(c, first, n), self.full(c, first, n), to, self.mine(0, 0, n))

    def keep(self, i, t, c, first):
        return pltpu.make_async_copy(self.mine(c, first, 1), self.full(c, first, 1), self.ksem.at[i])


def pump(net, s):
    z, y, x, d, end = net.z, net.y, net.x, net.d, net.end
    up, dn, xn, yn, cn = net.up, net.dn, net.xn, net.yn, net.cn
    a_u, a_d = 4 * x + 2 * y + 1, 4 * x + 2 * y
    b_u, b_d = 4 * y + 2, 4 * y
    c_u, c_d = 4, 0

    def z_reduce(base, k0, col, first_u, first_d, n):
        tu, td = s - (k0 + z), s - (k0 + 3 - z)
        cu, cd = 3 * tu + col, 3 * td + col
        net.add(base + ZU, tu, net.has_dn, cu, first_u, n, dn)
        net.pass_on(base + ZU, tu, net.has_up, cu, first_u, n, up)
        net.add(base + ZD, td, net.has_up, cd, first_d, n, up)
        net.pass_on(base + ZD, td, net.has_dn, cd, first_d, n, dn)

    def z_gather(base, k0, col, first_u, first_d, n, own):
        tu, td = s - (k0 + 3 - z), s - (k0 + z)
        cu, cd = 3 * tu + col, 3 * td + col
        mid = (z > 0) & (z < 3)
        net.got(base + GZU, tu, net.has_up, cu, first_u, n, up)
        if own:
            net.spread_own(base + GZU, tu, z == 3, cu, first_u, n, dn)
        net.spread(base + GZU, tu, mid if own else net.has_dn, cu, first_u, n, dn)
        net.got(base + GZD, td, net.has_dn, cd, first_d, n, dn)
        if own:
            net.spread_own(base + GZD, td, z == 0, cd, first_d, n, up)
        net.spread(base + GZD, td, mid if own else net.has_up, cd, first_d, n, up)

    t = s - 1
    net.pass_on(OA + X, t, None, 3 * t, 4 * (1 - x), 4, xn)
    net.pass_on(OB + Y, t, None, 3 * t + 1, 4 * (1 - y), 4, yn)
    z_reduce(OC, 1, 2, c_u, c_d, 4)
    t = s - 2
    net.add(OA + X, t, None, 3 * t, 4 * x, 4, xn)
    net.pass_on(OA + Y, t, None, 3 * t, 4 * x + 2 * (1 - y), 2, yn)
    net.add(OB + Y, t, None, 3 * t + 1, 4 * y, 4, yn)
    z_reduce(OB, 2, 1, b_u, b_d, 2)
    t = s - 3
    net.add(OA + Y, t, None, 3 * t, 4 * x + 2 * y, 2, yn)
    z_reduce(OA, 3, 0, a_u, a_d, 1)
    t = s - 4
    net.pass_on(OC + X, t, end, 3 * t + 2, 4 * d + 2 * (1 - x), 2, xn)
    t = s - 5
    net.add(OC + X, t, end, 3 * t + 2, 4 * d + 2 * x, 2, xn)
    net.pass_on(OC + Y, t, end, 3 * t + 2, 4 * d + 2 * x + 1 - y, 1, yn)
    net.pass_on(OB + X, t, end, 3 * t + 1, 4 * y + 2 * d + 1 - x, 1, xn)
    t = s - 6
    net.add(OC + Y, t, end, 3 * t + 2, 4 * d + 2 * x + y, 1, yn)
    net.add(OB + X, t, end, 3 * t + 1, 4 * y + 2 * d + x, 1, xn)
    own = [net.keep(0, t, 3 * t, 4 * x + 2 * y + d), net.keep(1, t, 3 * t + 1, 4 * y + 2 * d + x),
           net.keep(2, t, 3 * t + 2, 4 * d + 2 * x + y)]
    pl.when(net.ok(t, end))(lambda: [k.start() for k in own] and None)
    net.spread_own(OC + GY, t, end, 3 * t + 2, 4 * d + 2 * x + y, 1, yn)
    net.spread_own(OB + GX, t, end, 3 * t + 1, 4 * y + 2 * d + x, 1, xn)
    z_gather(OA, 6, 0, a_u, a_d, 1, True)
    pl.when(net.ok(t, end))(lambda: [k.wait() for k in own] and None)
    t = s - 7
    net.got(OC + GY, t, end, 3 * t + 2, 4 * d + 2 * x + 1 - y, 1, yn)
    net.spread(OC + GX, t, end, 3 * t + 2, 4 * d + 2 * x, 2, xn)
    net.got(OB + GX, t, end, 3 * t + 1, 4 * y + 2 * d + 1 - x, 1, xn)
    z_gather(OB, 7, 1, b_u, b_d, 2, False)
    t = s - 8
    net.got(OC + GX, t, end, 3 * t + 2, 4 * d + 2 * (1 - x), 2, xn)
    z_gather(OC, 8, 2, c_u, c_d, 4, False)
    t = s - 9
    net.spread(OA + GY, t, None, 3 * t, 4 * x + 2 * y, 2, yn)
    t = s - 10
    net.spread(OB + GY, t, None, 3 * t + 1, 4 * y, 4, yn)
    net.got(OA + GY, t, None, 3 * t, 4 * x + 2 * (1 - y), 2, yn)
    net.spread(OA + GX, t, None, 3 * t, 4 * x, 4, xn)
    t = s - 11
    net.got(OB + GY, t, None, 3 * t + 1, 4 * (1 - y), 4, yn)
    net.got(OA + GX, t, None, 3 * t, 4 * (1 - x), 4, xn)
    three = net.out.at[net.core, pl.ds(3 * t, 3)]
    net.send(DONE, t, None, three, three, cn, net.part.at[pl.ds(0, 3)])
    t = s - 12
    other = net.out.at[1 - net.core, pl.ds(3 * t, 3)]
    pl.when(net.ok(t))(lambda: net.copy(DONE, t, other, other, cn).wait_recv())


def exchange_kernel(scale, x_ref, y_ref, w1_ref, w2_ref, out_ref, h_ref, low_ref, saved_ref, w1_st, w2_st, gbuf, cslot, part,
                    wsem, ssem, rsem, csem, ksem, *slots):
    net = Net(part, out_ref, dict(zip(SLOT_PARTS, slots)), ssem, rsem, csem, ksem)
    core = net.core

    def weights(l):
        b = lax.rem(l, 2)
        return (pltpu.make_async_copy(w1_ref.at[l], w1_st.at[b], wsem.at[0, b]),
                pltpu.make_async_copy(w2_ref.at[l], w2_st.at[b], wsem.at[1, b]))

    def load(l):
        for c in weights(l):
            c.start()

    def loaded(l):
        for c in weights(l):
            c.wait()

    load(0)
    net.barrier()
    h_ref[...] = x_ref[...].astype(F32)

    @pl.loop(0, L)
    def _(l):
        pl.when(l < L - 1)(lambda: load(l + 1))
        loaded(l)
        b = lax.rem(l, 2)
        h_low = h_ref[...].astype(BF)
        saved_ref[l] = h_low
        tile = 512
        total = h_ref[...]
        for j in range(F // tile):
            w1 = w1_st[b, :, j * tile:(j + 1) * tile].astype(BF)
            act = gelu(dot(h_low, w1)).astype(BF)
            total = total + dot(act, w2_st[b, j * tile:(j + 1) * tile, :].astype(BF))
        h_ref[...] = total

    h_ref[...] = (h_ref[...] - y_ref[...].astype(F32)) * scale

    def backward(t, i):
        c = 3 * t + i
        l, j = L - 1 - c // TPL, lax.rem(c, TPL)
        b, col = lax.rem(l, 2), pl.multiple_of(j * FT, FT)

        @pl.when(j == 0)
        def _():
            pl.when(l < L - 2)(lambda: loaded(l))
            pl.when((l < L - 1) & (l > 0))(lambda: load(l - 1))
            low_ref[...] = h_ref[...].astype(BF)

        h_low, g_low = saved_ref[l], low_ref[...]
        w1 = w1_st[b, :, pl.ds(col, FT)].astype(BF)
        w2 = w2_st[b, pl.ds(col, FT), :].astype(BF)
        act, slope = gelu_both(dot(h_low, w1))
        q = (slope * dot(g_low, w2, 1, 1)).astype(BF)
        g2 = dot(act.astype(BF), g_low, 0, 0).astype(BF)
        g1 = dot(h_low, q, 0, 0).astype(BF)
        k = lax.rem(t, 2)
        gbuf[k, 0, i] = g1.reshape(8, PR, FT)
        gbuf[k, 1, i, 0:4] = g2[:, :FT].reshape(4, PR, FT)
        gbuf[k, 1, i, 4:8] = g2[:, FT:].reshape(4, PR, FT)
        h_ref[...] = h_ref[...] + dot(q, w1, 1, 1)

    def core_copy(t):
        return net.copy(CORE, t, gbuf.at[lax.rem(t, 2), 1 - core], net_slot(t), net.cn)

    def net_slot(t):
        return cslot.at[lax.rem(t, SLOTS)]

    def core_add(t):
        core_copy(t).wait_send()
        net.copy(CORE, t, net_slot(t), net_slot(t), net.cn).wait_recv()
        for i in range(3):
            part[lax.rem(3 * t + i, RING)] = gbuf[lax.rem(t, 2), core, i] + cslot[lax.rem(t, SLOTS), i]

    @pl.loop(0, NT + DEPTH)
    def _(s):
        pl.when(s >= LAG)(net.take_credit)
        pl.when(net.ok(s - 1))(lambda: core_add(s - 1))
        pump(net, s)

        @pl.when(net.ok(s))
        def _():
            @pl.loop(0, 3)
            def _(i):
                backward(s, i)
            core_copy(s).start()
        net.give_credit()

    for _ in range(LAG):
        net.take_credit()


def exchange(x_now, y_now, w_first, w_second, scale):
    vm = pl.BlockSpec(memory_space=pltpu.VMEM)
    hbm = pl.BlockSpec(memory_space=pl.ANY)
    return pl.pallas_call(
        functools.partial(exchange_kernel, scale),
        out_shape=jax.ShapeDtypeStruct((2, NC, 8, PR, FT), BF),
        in_specs=[vm, vm, hbm, hbm],
        out_specs=hbm,
        scratch_shapes=[
            pltpu.VMEM((R, D), F32), pltpu.VMEM((R, D), BF), pltpu.VMEM((L, R, D), BF),
            pltpu.VMEM((2, D, F), F32), pltpu.VMEM((2, F, D), F32),
            pltpu.VMEM((2, 2, 3, 8, PR, FT), BF), pltpu.VMEM((SLOTS, 3, 8, PR, FT), BF), pltpu.VMEM((RING, 8, PR, FT), BF),
            pltpu.SemaphoreType.DMA((2, 2)), pltpu.SemaphoreType.DMA((NTYPE, SLOTS)), pltpu.SemaphoreType.DMA((NTYPE, SLOTS)),
            pltpu.SemaphoreType.REGULAR((5,)), pltpu.SemaphoreType.DMA((3,)),
        ] + [pltpu.VMEM((SLOTS, n, PR, FT), BF) for n in SLOT_PARTS.values()],
        compiler_params=pltpu.CompilerParams(collective_id=0, has_side_effects=True, vmem_limit_bytes=63 * 2**20),
        name="exchange",
    )(x_now, y_now, w_first, w_second)


UT = 512


def update_kernel(rate, x_ref, g_ref, w1_ref, w2_ref, m1_ref, m2_ref, w1o, w2o, m1o, m2o, h_out, h_ref, low_ref):
    l, j = pl.program_id(0), pl.program_id(1)

    @pl.when((l == 0) & (j == 0))
    def _():
        h_ref[...] = x_ref[...].astype(F32)

    @pl.when(j == 0)
    def _():
        low_ref[...] = h_ref[...].astype(BF)

    n = UT // FT
    for k in range(n):
        cols = slice(k * FT, (k + 1) * FT)
        m = MOMENTUM * m1_ref[0, :, cols] + g_ref[0, k].reshape(D, FT).astype(F32)
        m1o[0, :, cols] = m
        w1o[0, :, cols] = w1_ref[0, :, cols] - rate * m
        for half in range(2):
            where = (0, slice(k * FT, (k + 1) * FT), slice(half * FT, (half + 1) * FT))
            m = MOMENTUM * m2_ref[where] + g_ref[1, k, 4 * half:4 * half + 4].reshape(FT, FT).astype(F32)
            m2o[where] = m
            w2o[where] = w2_ref[where] - rate * m
    act = gelu(dot(low_ref[...], w1o[0].astype(BF))).astype(BF)
    h_ref[...] = h_ref[...] + dot(act, w2o[0].astype(BF))

    @pl.when((l == L - 1) & (j == F // UT - 1))
    def _():
        h_out[...] = h_ref[...]


def update(x_next, grads, w_first, w_second, m_first, m_second, rate):
    tiles = F // UT
    first = pl.BlockSpec((1, D, UT), lambda l, j: (l, 0, j))
    second = pl.BlockSpec((1, UT, D), lambda l, j: (l, j, 0))
    whole = pl.BlockSpec((R, D), lambda l, j: (0, 0))
    chunks = pl.BlockSpec((2, UT // FT, 8, PR, FT), lambda l, j: (0, (L - 1 - l) * tiles + j, 0, 0, 0))
    return pl.pallas_call(
        functools.partial(update_kernel, rate),
        grid=(L, tiles),
        in_specs=[whole, chunks, first, second, first, second],
        out_specs=[first, second, first, second, whole],
        out_shape=[jax.ShapeDtypeStruct((L, D, F), F32), jax.ShapeDtypeStruct((L, F, D), F32)] * 2
        + [jax.ShapeDtypeStruct((R, D), F32)],
        scratch_shapes=[pltpu.VMEM((R, D), F32), pltpu.VMEM((R, D), BF)],
        compiler_params=pltpu.CompilerParams(vmem_limit_bytes=48 * 2**20, dimension_semantics=("arbitrary", "arbitrary")),
        cost_estimate=pl.CostEstimate(flops=4 * L * R * D * F, bytes_accessed=18 * 2 * L * D * F, transcendentals=L * R * F),
        name="update",
    )(x_next, grads, w_first, w_second, m_first, m_second)


def solution(mesh):
    rows_spec = P(("pod", "data"), None)
    full_spec = P()
    devices = mesh.shape["pod"] * mesh.shape["data"]

    def train_step(w_first, w_second, m_first, m_second, x_now, y_now, x_next, y_next):
        scale = 1.0 / (x_now.shape[0] * devices * D)
        grads = exchange(x_now, y_now, w_first, w_second, scale)
        w1, w2, m1, m2, hidden = update(x_next, grads, w_first, w_second, m_first, m_second, LEARN_BASE / L)
        resid = hidden - y_next.astype(F32)
        loss = jnp.sum(resid * resid, axis=-1) / (2 * D)
        return w1, w2, m1, m2, loss, hidden

    return jax.shard_map(train_step, mesh=mesh, in_specs=(full_spec,) * 4 + (rows_spec,) * 4,
                         out_specs=(full_spec,) * 4 + (P(("pod", "data")), rows_spec), check_vma=False)
```

time: 2280 us -> 564 us (0.25)
  waiting for transfers between devices: 1310 us -> 0 us
  Pallas kernels: 0 us -> 561 us
  matrix products: 402 us -> 0 us
  local copies, waits for them, and re-layouts: 312 us -> 0.01 us
  other arithmetic: 229 us -> 2.02 us
    reduce_scatter x24 -> x0, waiting for transfers between devices: 605 us -> none  [reduce_grad(): lax.psum_scatter(grad_low, 'data', scatter_dimension=scatter_dim, tiled=T...]
    pallas_call x0 -> x2, Pallas kernels: none -> 561 us  [the longest x1 404 us: exchange(): pl.pallas_call(functools.partial(exchange_kernel, scale), out_shape=jax.S...]
    psum x1 -> x0, waiting for transfers between devices: 446 us -> none  [reduce_grad(): shard_sum = lax.psum(shard_sum, 'pod')]
    dot_general x82 -> x0, matrix products: 402 us -> none  [the longest x12 130 us: train_step(): jnp.dot(act_low, weight_second.astype(jnp.bfloat16), preferred_element_ty...]
    unnamed x241 -> x4, local copies, waits for them, and re-layouts: 247 us -> 0.01 us
    all_gather x24 -> x0, waiting for transfers between devices: 244 us -> none  [reduce_grad(): lax.all_gather(shard_sum, 'data', axis=scatter_dim, tiled=True)]
    unnamed x22 -> x0, other arithmetic: 162 us -> none
    slice x2 -> x0, local copies, waits for them, and re-layouts: 66 us -> none  [the longest x1 33 us: train_step(): mom_first = MOMENTUM * m_first[layer_idx] + sum_first[layer_idx]]
  transfers between devices with their start and end apart: 49 -> 0, of which waited for: 32 -> 0; matrix products, arithmetic and copies ran while one was open for 22% -> 0% of each run, Pallas kernels for 0% -> 0%
where the time goes in v1:
time: 564 us
  Pallas kernels  561 us (99%)
    pallas_call x1, Pallas kernels, exchange(): pl.pallas_call(functools.partial(exchange_kernel, scale), out_shape=jax.S...  404 us
    pallas_call x1, Pallas kernels, update(): pl.pallas_call(functools.partial(update_kernel, rate), grid=(L, tiles), i...  158 us

profile of v1, /device:TPU:0, one launch (start us, length us, event | category | flops | bytes accessed | tf_op | source)
XLA Modules:
  0.0 564.0 jit_solution(5873157298999764020)
XLA Ops:
  0.6 0.0 copy-start
  0.6 403.6 %exchange.1.g_ref = bf16[2,96,8,64,256]{4,3,2,1,0:T(8,128)(2,1)} custom-call(bf16[512,512]{1,0:T(8,128)(2,1)} %x_ref.2, bf16[512,512]{1,0:T(8,128)(2,1)} %y_ref.1, f32[12,512,2048]{2,1,0:T(8,128)} %w1_ref.3, f32[12,2048,512]{2,1,0:T(8,128)} %w2_ref.3), custom_call_target="tpu_custom_call" | custom-call | tf_op jit(solution)/shard_map/exchange/pallas_call | solution.py:310
  404.2 0.0 copy-done
  404.2 0.0 copy-start.1
  404.2 157.8 %update.1 = (f32[12,512,2048]{2,1,0:T(8,128)}, f32[12,2048,512]{2,1,0:T(8,128)}, f32[12,512,2048]{2,1,0:T(8,128)}, f32[12,2048,512]{2,1,0:T(8,128)}, f32[512,512]{1,0:T(8,128)}) custom-call(bf16[512,512]{1,0:T(8,128)(2,1)S(1)} %copy-done, bf16[2,96,8,64,256]{4,3,2,1,0:T(8,128)(2,1)} %exchange.1.g_ref, f32[12,512,2048]{2,1,0:T(8,128)} %w1_ref.3, ...), custom_call_target="tpu_custom_call" | custom-call | flops 25769803776 | bytes 452984832 | tf_op jit(solution)/shard_map/update/pallas_call | solution.py:366
  562.0 0.0 copy-done.1
  562.0 1.4 multiply_reduce_fusion
  563.5 0.6 broadcast_multiply_fusion
Async XLA Ops:
  0.6 403.6 %copy-start = (bf16[512,512]{1,0:T(8,128)(2,1)S(1)}, bf16[512,512]{1,0:T(8,128)(2,1)}, u32[]{:S(2)}) copy-start(bf16[512,512]{1,0:T(8,128)(2,1)} %x_ref.3) | copy-start | bytes 1572868
  404.2 157.8 %copy-start.1 = (bf16[512,512]{1,0:T(8,128)(2,1)S(1)}, bf16[512,512]{1,0:T(8,128)(2,1)}, u32[]{:S(2)}) copy-start(bf16[512,512]{1,0:T(8,128)(2,1)} %param.15) | copy-start | bytes 1572868

commit v2 on v0

v2 whole, which is shorter than its diff:
```python
import functools

import jax
import jax.numpy as jnp
from jax import lax
from jax.experimental import pallas as pl
from jax.experimental.pallas import tpu as pltpu
from jax.sharding import PartitionSpec as P

MESH = pl.DeviceIdType.MESH
LEARN_BASE = 0.25
MOMENTUM = 0.9
GELU_C = 0.7978845608028654
GELU_A = 0.044715
BF, F32 = jnp.bfloat16, jnp.float32

L, D, F, R = 12, 512, 2048, 512
FT = 256
TPL = F // FT
NC = L * TPL
NT = NC // 3
LN = 128
TR = 3 * D * FT // LN
RING = 12
SLOTS, LAG, DEPTH = 4, 2, 15

CORE, DONE, OA, OB, OC, NTYPE = 0, 1, 2, 10, 20, 30
X, Y, ZU, ZD, GZU, GZD, GY, GX, W, GW = range(10)
FIRST_ROW = {OA: 0, OB: 1280, OC: 2176}
PART_ROWS = {OA: 160, OB: 112, OC: 112}
SLOT_ROWS = {}
for _base, _order in ((OA, "xyz"), (OB, "yzx"), (OC, "zxy")):
    for _n, _ax in zip((4, 2, 1), _order):
        for _ty in {"x": (X,), "y": (Y,), "z": (ZU, ZD) if _base == OA else (ZU, ZD, W)}[_ax]:
            SLOT_ROWS[_base + _ty] = _n * PART_ROWS[_base]


def gelu(a):
    return 0.5 * a * (1.0 + jnp.tanh(GELU_C * (a + GELU_A * (a * a * a))))


def gelu_both(a):
    sq = a * a
    th = jnp.tanh(GELU_C * (a + GELU_A * (sq * a)))
    half = 0.5 * (1.0 + th)
    slope = half + 0.5 * a * (1.0 - th * th) * (GELU_C * (1.0 + 3.0 * GELU_A * sq))
    return a * half, slope


def dot(a, b, da=1, db=0):
    return lax.dot_general(a, b, (((da,), (db,)), ((), ())), preferred_element_type=F32)


class Net:
    def __init__(self, part, out, slots, ssem, rsem, csem, ksem):
        self.part, self.out, self.slots = part, out, slots
        self.ssem, self.rsem, self.csem, self.ksem = ssem, rsem, csem, ksem
        pod, data = lax.axis_index("pod"), lax.axis_index("data")
        z, y, x, core = pod // 2, lax.rem(pod, 2), data // 2, lax.rem(data, 2)
        self.z, self.y, self.x, self.core = z, y, x, core
        self.at = lambda z: (z * 2 + y, x * 2 + core)
        self.xn, self.yn, self.cn = (pod, 2 * (1 - x) + core), (z * 2 + 1 - y, data), (pod, 2 * x + 1 - core)
        self.up, self.dn = self.at(z + 1), self.at(z - 1)
        self.cross = self.at(jnp.where(lax.rem(z, 2) == 0, z + 1, z - 1))
        self.d = z // 2
        self.sent = []

    def neighbours(self):
        return ((self.xn, None), (self.yn, None), (self.cn, None), (self.up, self.z < 3), (self.dn, self.z > 0))

    def each(self, fn):
        for i, (n, cond) in enumerate(self.neighbours()):
            go = functools.partial(fn, i, n)
            if cond is None:
                go()
            else:
                pl.when(cond)(go)

    def greet(self):
        sem = pltpu.get_barrier_semaphore()
        self.each(lambda i, n: pl.semaphore_signal(sem, inc=1, device_id=n, device_id_type=MESH))

    def greeted(self):
        pl.semaphore_wait(pltpu.get_barrier_semaphore(), 3 + jnp.where(self.z < 3, 1, 0) + jnp.where(self.z > 0, 1, 0))

    def give_credit(self):
        file = (0, 1, 2, 4, 3)
        self.each(lambda i, n: pl.semaphore_signal(self.csem.at[file[i]], inc=1, device_id=n, device_id_type=MESH))

    def take_credit(self):
        self.each(lambda i, n: pl.semaphore_wait(self.csem.at[i], 1))

    def copy(self, ty, t, src, dst, to):
        s = lax.rem(t, SLOTS)
        return pltpu.make_async_remote_copy(src_ref=src, dst_ref=dst, send_sem=self.ssem.at[ty, s], recv_sem=self.rsem.at[ty, s],
                                            device_id=to, device_id_type=MESH)

    def slot(self, ty, t):
        return self.slots[ty].at[lax.rem(t, SLOTS)]

    def rows(self, base, first, n):
        return pl.ds(pl.multiple_of(FIRST_ROW[base] + first * PART_ROWS[base], 16), n * PART_ROWS[base])

    def mine(self, base, t, first, n):
        return self.part.at[lax.rem(t, RING), self.rows(base, first, n)]

    def full(self, base, t, first, n):
        return self.out.at[self.core, t, self.rows(base, first, n)]

    def send(self, ty, t, src, dst, to, like, cond=None):
        pl.when(t >= SLOTS)(lambda: self.copy(ty, t - SLOTS, like(), like(), to).wait_send())
        self.copy(ty, t, src, dst, to).start()
        self.sent.append((ty, like, to, cond))

    def all_sent(self):
        for ty, like, to, cond in self.sent:
            for t in (NT - 4, NT - 3):
                def go(t=t):
                    for u in (t, t + 2):
                        self.copy(ty, u, like(), like(), to).wait_send()
                if cond is None:
                    go()
                else:
                    pl.when(cond(t))(go)

    def add(self, base, kind, t, first, n, frm):
        got = self.slot(base + kind, t)
        self.copy(base + kind, t, got, got, frm).wait_recv()
        row, rows = lax.rem(t, RING), self.rows(base, first, n)
        self.part[row, rows] = self.part[row, rows] + got[...]

    def pass_on(self, base, kind, t, first, n, to, cond=None):
        self.send(base + kind, t, self.mine(base, t, first, n), self.slot(base + kind, t), to, lambda: self.mine(base, 0, 0, n), cond)

    def got(self, base, kind, t, first, n, frm):
        ref = self.full(base, t, first, n)
        self.copy(base + kind, t, ref, ref, frm).wait_recv()

    def spread(self, base, kind, t, first, n, to, cond=None, own=False):
        full = self.full(base, t, first, n)
        self.send(base + kind, t, self.mine(base, t, first, n) if own else full, full, to, lambda: self.mine(base, 0, 0, n), cond)

    def keep(self, i, base, t, first):
        return pltpu.make_async_copy(self.mine(base, t, first, 1), self.full(base, t, first, 1), self.ksem.at[i])


class Momentum:
    def __init__(self, out, old, new, tiles, grads, sems):
        self.out, self.old, self.new, self.tiles, self.grads, self.sems = out, old, new, tiles, grads, sems

    def copies(self, t, back):
        k = lax.rem(t, 2)
        for i in range(3):
            c = 3 * t + i
            l, cols = L - 1 - c // TPL, pl.ds(pl.multiple_of(lax.rem(c, TPL) * FT, FT), FT)
            for w, where in enumerate(((l, slice(None), cols), (l, cols))):
                tile, sem = self.tiles[w].at[k, i], self.sems.at[int(back), w, k, i]
                if back:
                    yield pltpu.make_async_copy(tile, self.new[w].at[where], sem)
                else:
                    yield pltpu.make_async_copy(self.old[w].at[where], tile, sem)
        if not back:
            yield pltpu.make_async_copy(self.out.at[:, t], self.grads.at[k], self.sems.at[2, 0, k, 0])

    def load(self, t):
        for c in self.copies(t, False):
            c.start()

    def update(self, t):
        for c in self.copies(t, False):
            c.wait()
        k = lax.rem(t, 2)
        for i in range(3):
            row = i * (TR // 3)
            for w, (tile, n) in enumerate(zip(self.tiles, (D, FT))):
                for q in range(TR // 3 // n):
                    cols = slice(q * LN, (q + 1) * LN)
                    tile[k, i, :, cols] = MOMENTUM * tile[k, i, :, cols] + self.grads[k, w, row + q * n:row + (q + 1) * n].astype(F32)
        for c in self.copies(t, True):
            c.start()

    def stored(self, t):
        for c in self.copies(t, True):
            c.wait()


def valid(t):
    return (t >= 0) & (t < NT)


def pump(net, s, compute, momentum):
    z, y, x, d = net.z, net.y, net.x, net.d
    up, dn, xn, yn, cn, cross = net.up, net.dn, net.xn, net.yn, net.cn, net.cross
    side = lambda: (z == 0) | (z == 3)

    def mode(base, t):
        if base == OA:
            return 0
        return t % 2 if isinstance(t, int) else lax.rem(t, 2)

    def owner(base):
        return lambda t: z == 3 * d + mode(base, t) * (1 - 2 * d)

    def if_(t, cond, *acts):
        @pl.when(cond(t))
        def _():
            for act in acts:
                act()

    def stage(k, fn):
        t = s - k
        pl.when(valid(t))(lambda: fn(t))

    def add(*a):
        return lambda: net.add(*a)

    def got(*a):
        return lambda: net.got(*a)

    def pass_on(*a):
        return lambda: net.pass_on(*a)

    def spread(*a, **k):
        return lambda: net.spread(*a, **k)

    def z_reduce(base, k0, first_u, first_d, n):
        def climb(t):
            to_up = lambda t: z < 3 - mode(base, t)
            if_(t, lambda t: (z > 0) & (z <= 3 - mode(base, t)), add(base, ZU, t, first_u, n, dn))
            if_(t, to_up, pass_on(base, ZU, t, first_u, n, up, to_up))

        def sink(t):
            to_dn = lambda t: z > mode(base, t)
            if_(t, lambda t: (z < 3) & (z >= mode(base, t)), add(base, ZD, t, first_d, n, up))
            if_(t, to_dn, pass_on(base, ZD, t, first_d, n, dn, to_dn))

        stage(k0 + z, climb)
        stage(k0 + 3 - z, sink)
        if base != OA:
            f = jnp.where(z >= 2, first_u, first_d)
            give = lambda t: side() & (mode(base, t) == 1)
            stage(k0, lambda t: if_(t, give, pass_on(base, W, t, f, n, cross, give)))
            stage(k0 + 1, lambda t: if_(t, lambda t: ~side() & (mode(base, t) == 1), add(base, W, t, f, n, cross)))

    def z_gather(base, k0, first_u, first_d, n):
        own = base == OA

        def sink(t):
            to_dn = lambda t: (z > 0) & (z <= (2 if own else 3 - mode(base, t)))
            if_(t, lambda t: z < 3 - mode(base, t), got(base, GZU, t, first_u, n, up))
            if own:
                top = lambda t: z == 3
                if_(t, top, spread(base, GZU, t, first_u, n, dn, top, own=True))
            if_(t, to_dn, spread(base, GZU, t, first_u, n, dn, to_dn))

        def climb(t):
            to_up = lambda t: (z < 3) & (z >= (1 if own else mode(base, t)))
            if_(t, lambda t: z > mode(base, t), got(base, GZD, t, first_d, n, dn))
            if own:
                bottom = lambda t: z == 0
                if_(t, bottom, spread(base, GZD, t, first_d, n, up, bottom, own=True))
            if_(t, to_up, spread(base, GZD, t, first_d, n, up, to_up))

        stage(k0 + 3 - z, sink)
        stage(k0 + z, climb)
        if not own:
            f = jnp.where(z >= 2, first_u, first_d)
            give = lambda t: ~side() & (mode(base, t) == 1)
            stage(k0 + 1, lambda t: if_(t, give, spread(base, GW, t, f, n, cross, give)))
            stage(k0 + 2, lambda t: if_(t, lambda t: side() & (mode(base, t) == 1), got(base, GW, t, f, n, cross)))

    own_a, own_b, own_c = 4 * x + 2 * y + d, 4 * y + 2 * d + x, 4 * d + 2 * x + y

    def kept(t):
        for i, (base, first) in enumerate(((OA, own_a), (OB, own_b), (OC, own_c))):
            if_(t, owner(base), net.keep(i, base, t, first).wait)

    def k1(t):
        net.pass_on(OA, X, t, 4 * (1 - x), 4, xn)
        net.pass_on(OB, Y, t, 4 * (1 - y), 4, yn)

    def k2(t):
        net.add(OA, X, t, 4 * x, 4, xn)
        net.pass_on(OA, Y, t, 4 * x + 2 * (1 - y), 2, yn)
        net.add(OB, Y, t, 4 * y, 4, yn)

    def k4(t):
        if_(t, owner(OC), pass_on(OC, X, t, 4 * d + 2 * (1 - x), 2, xn, owner(OC)))

    def k5(t):
        if_(t, owner(OC), add(OC, X, t, 4 * d + 2 * x, 2, xn),
            pass_on(OC, Y, t, 4 * d + 2 * x + 1 - y, 1, yn, owner(OC)))
        if_(t, owner(OB), pass_on(OB, X, t, 4 * y + 2 * d + 1 - x, 1, xn, owner(OB)))

    def k6(t):
        if_(t, owner(OC), add(OC, Y, t, own_c, 1, yn), net.keep(2, OC, t, own_c).start,
            spread(OC, GY, t, own_c, 1, yn, owner(OC), own=True))
        if_(t, owner(OB), add(OB, X, t, own_b, 1, xn), net.keep(1, OB, t, own_b).start,
            spread(OB, GX, t, own_b, 1, xn, owner(OB), own=True))

    def k7(t):
        if_(t, owner(OC), got(OC, GY, t, 4 * d + 2 * x + 1 - y, 1, yn), spread(OC, GX, t, 4 * d + 2 * x, 2, xn, owner(OC)))
        if_(t, owner(OB), got(OB, GX, t, 4 * y + 2 * d + 1 - x, 1, xn))

    def k10(t):
        net.spread(OB, GY, t, 4 * y, 4, yn)
        net.got(OA, GY, t, 4 * x + 2 * (1 - y), 2, yn)
        net.spread(OA, GX, t, 4 * x, 4, xn)

    def k11(t):
        net.got(OB, GY, t, 4 * (1 - y), 4, yn)
        net.got(OA, GX, t, 4 * (1 - x), 4, xn)
        triple = net.out.at[net.core, t]
        net.send(DONE, t, triple, triple, cn, lambda: net.part.at[0])

    def k12(t):
        other = net.out.at[1 - net.core, t]
        net.copy(DONE, t, other, other, cn).wait_recv()

    stage(7, kept)
    stage(1, k1)
    z_reduce(OC, 1, 4, 0, 4)
    compute(0)
    stage(2, k2)
    z_reduce(OB, 2, 4 * y + 2, 4 * y, 2)
    stage(3, lambda t: net.add(OA, Y, t, 4 * x + 2 * y, 2, yn))
    z_reduce(OA, 3, 4 * x + 2 * y + 1, 4 * x + 2 * y, 1)
    stage(4, k4)
    stage(5, k5)
    compute(1)
    stage(6, k6)
    stage(6, lambda t: if_(t, owner(OA), net.keep(0, OA, t, own_a).start))
    z_gather(OA, 6, 4 * x + 2 * y + 1, 4 * x + 2 * y, 1)
    stage(7, k7)
    z_gather(OB, 7, 4 * y + 2, 4 * y, 2)
    stage(8, lambda t: if_(t, owner(OC), got(OC, GX, t, 4 * d + 2 * (1 - x), 2, xn)))
    z_gather(OC, 8, 4, 0, 4)
    compute(2)
    stage(9, lambda t: net.spread(OA, GY, t, 4 * x + 2 * y, 2, yn))
    stage(10, k10)
    stage(11, k11)
    stage(14, momentum.stored)
    stage(12, k12)
    stage(12, momentum.load)
    stage(13, momentum.update)


def exchange_kernel(scale, x_ref, y_ref, w1_ref, w2_ref, m1_ref, m2_ref, out_ref, m1_new, m2_new, h_ref, low_ref, turn_ref, saved_ref, w1_st, w2_st, gbuf, cslot, part,
                    tile1, tile2, grads, wsem, psem, msem, ssem, rsem, csem, ksem, *slots):
    net = Net(part, out_ref, dict(zip(SLOT_ROWS, slots)), ssem, rsem, csem, ksem)
    core = net.core
    momentum = Momentum(out_ref, (m1_ref, m2_ref), (m1_new, m2_new), (tile1, tile2), grads, msem)

    half = F // 2

    def weights(i):
        b, cols = lax.rem(i, 4), pl.ds(pl.multiple_of(lax.rem(i, 2) * half, half), half)
        return (pltpu.make_async_copy(w1_ref.at[i // 2, :, cols], w1_st.at[b], wsem.at[0, b]),
                pltpu.make_async_copy(w2_ref.at[i // 2, cols, :], w2_st.at[b], wsem.at[1, b]))

    def load(i):
        for c in weights(i):
            c.start()

    def loaded(i):
        for c in weights(i):
            c.wait()

    net.greet()
    for i in range(3):
        load(i)
    h_ref[...] = x_ref[...].astype(F32)

    @pl.loop(0, 2 * L)
    def _(i):
        pl.when(i < 2 * L - 3)(lambda: load(i + 3))
        l, b = i // 2, lax.rem(i, 4)

        @pl.when(lax.rem(i, 2) == 0)
        def _():
            saved_ref[l] = h_ref[...].astype(BF)
        loaded(i)
        act = gelu(dot(saved_ref[l], w1_st[b].astype(BF))).astype(BF)
        h_ref[...] = h_ref[...] + dot(act, w2_st[b].astype(BF))

    h_ref[...] = (h_ref[...] - y_ref[...].astype(F32)) * scale

    def backward(t, i):
        c = 3 * t + i
        l, j = L - 1 - c // TPL, lax.rem(c, TPL)
        i0 = 2 * l
        b, col = lax.rem(i0 + j // (TPL // 2), 4), pl.multiple_of(lax.rem(j, TPL // 2) * FT, FT)

        def piece(l):
            i = 2 * l + j // (TPL // 2)
            b, to = lax.rem(i, 4), pl.ds(col, FT)
            frm = pl.ds(pl.multiple_of(j * FT, FT), FT)
            return (pltpu.make_async_copy(w1_ref.at[l, :, frm], w1_st.at[b, :, to], psem.at[0, lax.rem(l, 2), j]),
                    pltpu.make_async_copy(w2_ref.at[l, frm, :], w2_st.at[b, to, :], psem.at[1, lax.rem(l, 2), j]))

        @pl.when((l < L - 1) & (l > 0))
        def _():
            for p in piece(l - 1):
                p.start()

        @pl.when(l < L - 2)
        def _():
            for p in piece(l):
                p.wait()

        @pl.when(j == 0)
        def _():
            low_ref[...] = h_ref[...].astype(BF)
            turn_ref[...] = saved_ref[l].T

        h_low, g_low = saved_ref[l], low_ref[...]
        w1 = w1_st[b, :, pl.ds(col, FT)].astype(BF)
        w2 = w2_st[b, pl.ds(col, FT), :].astype(BF)
        act, slope = gelu_both(dot(h_low, w1))
        q = (slope * dot(g_low, w2, 1, 1)).astype(BF)
        g2 = dot(act.astype(BF), g_low, 0, 0).astype(BF)
        g1 = dot(turn_ref[...], q).astype(BF)
        k, row = lax.rem(t, 2), i * (TR // 3)
        for half in range(FT // LN):
            gbuf[k, 0, pl.ds(row + half * D, D)] = g1[:, half * LN:(half + 1) * LN]
        for q4 in range(D // LN):
            gbuf[k, 1, pl.ds(row + q4 * FT, FT)] = g2[:, q4 * LN:(q4 + 1) * LN]
        h_ref[...] = h_ref[...] + dot(q, w1, 1, 1)

    def core_copy(t):
        return net.copy(CORE, t, gbuf.at[lax.rem(t, 2), 1 - core], net_slot(t), net.cn)

    def net_slot(t):
        return cslot.at[lax.rem(t, SLOTS)]

    def core_add(t):
        core_copy(t).wait_send()
        net.copy(CORE, t, net_slot(t), net_slot(t), net.cn).wait_recv()
        part[lax.rem(t, RING)] = gbuf[lax.rem(t, 2), core] + cslot[lax.rem(t, SLOTS)]

    net.greeted()

    @pl.loop(0, NT + DEPTH)
    def _(s):
        pl.when(s >= LAG)(net.take_credit)
        pl.when(valid(s - 1))(lambda: core_add(s - 1))
        def compute(i):
            @pl.when(valid(s))
            def _():
                backward(s, i)
                if i == 2:
                    core_copy(s).start()

        pump(net, s, compute, momentum)
        net.give_credit()

    net.all_sent()
    for _ in range(LAG):
        net.take_credit()


def exchange(x_now, y_now, w_first, w_second, m_first, m_second, scale):
    vm = pl.BlockSpec(memory_space=pltpu.VMEM)
    hbm = pl.BlockSpec(memory_space=pl.ANY)
    return pl.pallas_call(
        functools.partial(exchange_kernel, scale),
        out_shape=[jax.ShapeDtypeStruct((2, NT, TR, LN), BF), jax.ShapeDtypeStruct((L, D, F), F32),
                   jax.ShapeDtypeStruct((L, F, D), F32)],
        in_specs=[vm, vm] + [hbm] * 4,
        out_specs=[hbm] * 3,
        scratch_shapes=[
            pltpu.VMEM((R, D), F32), pltpu.VMEM((R, D), BF), pltpu.VMEM((D, R), BF), pltpu.VMEM((L, R, D), BF),
            pltpu.VMEM((4, D, F // 2), F32), pltpu.VMEM((4, F // 2, D), F32),
            pltpu.VMEM((2, 2, TR, LN), BF), pltpu.VMEM((SLOTS, TR, LN), BF), pltpu.VMEM((RING, TR, LN), BF),
            pltpu.VMEM((2, 3, D, FT), F32), pltpu.VMEM((2, 3, FT, D), F32), pltpu.VMEM((2, 2, TR, LN), BF),
            pltpu.SemaphoreType.DMA((2, 4)), pltpu.SemaphoreType.DMA((2, 2, TPL)), pltpu.SemaphoreType.DMA((3, 2, 2, 3)), pltpu.SemaphoreType.DMA((NTYPE, SLOTS)), pltpu.SemaphoreType.DMA((NTYPE, SLOTS)),
            pltpu.SemaphoreType.REGULAR((5,)), pltpu.SemaphoreType.DMA((3,)),
        ] + [pltpu.VMEM((SLOTS, n, LN), BF) for n in SLOT_ROWS.values()],
        compiler_params=pltpu.CompilerParams(collective_id=0, has_side_effects=True, vmem_limit_bytes=63 * 2**20),
        name="exchange",
    )(x_now, y_now, w_first, w_second, m_first, m_second)


UT = 512
TILES = F // UT
BUFS, AHEAD = 8, 4


def update_kernel(rate, x_ref, w1_ref, w2_ref, m1_ref, m2_ref, w1o, w2o, m1o, m2o, h_ref, low_ref, w1, w2, m1, m2, isem, osem):
    olds, news, tiles = (w1_ref, w2_ref, m1_ref, m2_ref), (w1o, w2o, m1o, m2o), (w1, w2, m1, m2)

    def copy(a, i, back):
        l, cols = i // TILES, pl.ds(pl.multiple_of(lax.rem(i, TILES) * UT, UT), UT)
        where = (l, slice(None), cols) if a % 2 == 0 else (l, cols)
        k = lax.rem(i, BUFS)
        if back:
            return pltpu.make_async_copy(tiles[a].at[k], news[a].at[where], osem.at[a, k])
        return pltpu.make_async_copy(olds[a].at[where], tiles[a].at[k], isem.at[a, k])

    def load(i):
        for a in range(4):
            copy(a, i, False).start()

    def stored(i):
        for a in range(4):
            copy(a, i, True).wait()

    for i in range(AHEAD):
        load(i)
    h_ref[...] = x_ref[...].astype(F32)

    @pl.loop(0, L * TILES)
    def _(i):
        pl.when(i + AHEAD >= BUFS)(lambda: pl.when(i + AHEAD < L * TILES)(lambda: stored(i + AHEAD - BUFS)))
        pl.when(i + AHEAD < L * TILES)(lambda: load(i + AHEAD))

        @pl.when(lax.rem(i, TILES) == 0)
        def _():
            low_ref[...] = h_ref[...].astype(BF)

        for a in range(4):
            copy(a, i, False).wait()
        for a in (2, 3):
            copy(a, i, True).start()
        k = lax.rem(i, BUFS)
        first = w1[k] - rate * m1[k]
        w1[k] = first
        copy(0, i, True).start()
        act = gelu(dot(low_ref[...], first.astype(BF))).astype(BF)
        second = w2[k] - rate * m2[k]
        w2[k] = second
        copy(1, i, True).start()
        h_ref[...] = h_ref[...] + dot(act, second.astype(BF))

    @pl.loop(L * TILES - BUFS, L * TILES)
    def _(i):
        stored(i)


def update(x_next, w_first, w_second, m_first, m_second, rate):
    vm = pl.BlockSpec(memory_space=pltpu.VMEM)
    hbm = pl.BlockSpec(memory_space=pl.ANY)
    return pl.pallas_call(
        functools.partial(update_kernel, rate),
        in_specs=[vm] + [hbm] * 4,
        out_specs=[hbm] * 4 + [vm],
        out_shape=[jax.ShapeDtypeStruct((L, D, F), F32), jax.ShapeDtypeStruct((L, F, D), F32)] * 2
        + [jax.ShapeDtypeStruct((R, D), F32)],
        scratch_shapes=[pltpu.VMEM((R, D), BF)] + [pltpu.VMEM((BUFS, D, UT), F32), pltpu.VMEM((BUFS, UT, D), F32)] * 2
        + [pltpu.SemaphoreType.DMA((4, BUFS))] * 2,
        compiler_params=pltpu.CompilerParams(vmem_limit_bytes=60 * 2**20),
        cost_estimate=pl.CostEstimate(flops=4 * L * R * D * F, bytes_accessed=16 * 2 * L * D * F, transcendentals=L * R * F),
        name="update",
    )(x_next, w_first, w_second, m_first, m_second)


def solution(mesh):
    rows_spec = P(("pod", "data"), None)
    full_spec = P()
    devices = mesh.shape["pod"] * mesh.shape["data"]

    def train_step(w_first, w_second, m_first, m_second, x_now, y_now, x_next, y_next):
        scale = 1.0 / (x_now.shape[0] * devices * D)
        _, m_first, m_second = exchange(x_now, y_now, w_first, w_second, m_first, m_second, scale)
        w1, w2, m1, m2, hidden = update(x_next, w_first, w_second, m_first, m_second, LEARN_BASE / L)
        resid = hidden - y_next.astype(F32)
        loss = jnp.sum(resid * resid, axis=-1) / (2 * D)
        return w1, w2, m1, m2, loss, hidden

    return jax.shard_map(train_step, mesh=mesh, in_specs=(full_spec,) * 4 + (rows_spec,) * 4,
                         out_specs=(full_spec,) * 4 + (P(("pod", "data")), rows_spec), check_vma=False)
```

time: 2280 us -> 533 us (0.23)
  waiting for transfers between devices: 1310 us -> 0 us
  Pallas kernels: 0 us -> 530 us
  matrix products: 402 us -> 0 us
  local copies, waits for them, and re-layouts: 312 us -> 0.01 us
  other arithmetic: 229 us -> 2.02 us
    reduce_scatter x24 -> x0, waiting for transfers between devices: 605 us -> none  [reduce_grad(): lax.psum_scatter(grad_low, 'data', scatter_dimension=scatter_dim, tiled=T...]
    pallas_call x0 -> x2, Pallas kernels: none -> 530 us  [the longest x1 399 us: exchange(): pl.pallas_call(functools.partial(exchange_kernel, scale), out_shape=[jax....]
    psum x1 -> x0, waiting for transfers between devices: 446 us -> none  [reduce_grad(): shard_sum = lax.psum(shard_sum, 'pod')]
    dot_general x82 -> x0, matrix products: 402 us -> none  [the longest x12 130 us: train_step(): jnp.dot(act_low, weight_second.astype(jnp.bfloat16), preferred_element_ty...]
    unnamed x241 -> x2, local copies, waits for them, and re-layouts: 247 us -> 0.01 us
    all_gather x24 -> x0, waiting for transfers between devices: 244 us -> none  [reduce_grad(): lax.all_gather(shard_sum, 'data', axis=scatter_dim, tiled=True)]
    unnamed x22 -> x0, other arithmetic: 162 us -> none
    slice x2 -> x0, local copies, waits for them, and re-layouts: 66 us -> none  [the longest x1 33 us: train_step(): mom_first = MOMENTUM * m_first[layer_idx] + sum_first[layer_idx]]
  transfers between devices with their start and end apart: 49 -> 0, of which waited for: 32 -> 0; matrix products, arithmetic and copies ran while one was open for 22% -> 0% of each run, Pallas kernels for 0% -> 0%
where the time goes in v2:
time: 533 us; the launch traced here: 532 us
  Pallas kernels  530 us (99%)
    pallas_call x1, Pallas kernels, exchange(): pl.pallas_call(functools.partial(exchange_kernel, scale), out_shape=[jax....  399 us
    pallas_call x1, Pallas kernels, update(): pl.pallas_call(functools.partial(update_kernel, rate), in_specs=[vm] + [h...  130 us

profile of v2, /device:TPU:0, one launch (start us, length us, event | category | flops | bytes accessed | tf_op | source)
XLA Modules:
  0.0 532.4 jit_solution(15733178426742940827)
XLA Ops:
  0.6 399.3 %exchange.1 = (bf16[2,32,3072,128]{3,2,1,0:T(8,128)(2,1)}, f32[12,512,2048]{2,1,0:T(8,128)}, f32[12,2048,512]{2,1,0:T(8,128)}) custom-call(bf16[512,512]{1,0:T(8,128)(2,1)} %x_ref.2, bf16[512,512]{1,0:T(8,128)(2,1)} %y_ref.1, f32[12,512,2048]{2,1,0:T(8,128)} %w1_ref.3, f32[12,2048,512]{2,1,0:T(8,128)} %w2_ref.3, f32[12,512,2048]{2,1,0:T(8,128)} %m1_ref.1, ...), custom_call_target="tpu_custom_call" | custom-call | tf_op jit(solution)/shard_map/exchange/pallas_call | solution.py:465
  399.9 0.0 copy-start
  399.9 130.4 %update.1 = (f32[12,512,2048]{2,1,0:T(8,128)}, f32[12,2048,512]{2,1,0:T(8,128)}, f32[12,512,2048]{2,1,0:T(8,128)}, f32[12,2048,512]{2,1,0:T(8,128)}, f32[512,512]{1,0:T(8,128)}) custom-call(bf16[512,512]{1,0:T(8,128)(2,1)} %x_ref.3, f32[12,512,2048]{2,1,0:T(8,128)} %w1_ref.3, f32[12,2048,512]{2,1,0:T(8,128)} %w2_ref.3, ...), custom_call_target="tpu_custom_call" | custom-call | flops 25769803776 | bytes 402653184 | tf_op jit(solution)/shard_map/update/pallas_call | solution.py:543
  530.4 0.0 copy-done
  530.4 1.4 multiply_reduce_fusion
  531.8 0.6 broadcast_multiply_fusion
Async XLA Ops:
  399.9 130.5 %copy-start = (bf16[512,512]{1,0:T(8,128)(2,1)S(1)}, bf16[512,512]{1,0:T(8,128)(2,1)}, u32[]{:S(2)}) copy-start(bf16[512,512]{1,0:T(8,128)(2,1)} %param.15) | copy-start | bytes 1572868

commit v3 on v2

--- a/solution.py
+++ b/solution.py
@@ -31,7 +31,7 @@
 SLOT_ROWS = {}
 for _base, _order in ((OA, "xyz"), (OB, "yzx"), (OC, "zxy")):
     for _n, _ax in zip((4, 2, 1), _order):
-        for _ty in {"x": (X,), "y": (Y,), "z": (ZU, ZD) if _base == OA else (ZU, ZD, W)}[_ax]:
+        for _ty in {"x": (X,), "y": (Y,), "z": (ZU, ZD, W) if _base == OC else (ZU, ZD)}[_ax]:
             SLOT_ROWS[_base + _ty] = _n * PART_ROWS[_base]
 
 
@@ -108,16 +108,20 @@
         return self.out.at[self.core, t, self.rows(base, first, n)]
 
     def send(self, ty, t, src, dst, to, like, cond=None):
-        pl.when(t >= SLOTS)(lambda: self.copy(ty, t - SLOTS, like(), like(), to).wait_send())
+        if cond is None:
+            self.wait_old(ty, t, like, to)
         self.copy(ty, t, src, dst, to).start()
         self.sent.append((ty, like, to, cond))
 
+    def wait_old(self, ty, t, like, to, cond=None):
+        was = t >= SLOTS if cond is None else (t >= SLOTS) & cond(t - SLOTS)
+        pl.when(was)(lambda: self.copy(ty, t - SLOTS, like(), like(), to).wait_send())
+
     def all_sent(self):
         for ty, like, to, cond in self.sent:
-            for t in (NT - 4, NT - 3):
+            for t in range(NT - SLOTS, NT):
                 def go(t=t):
-                    for u in (t, t + 2):
-                        self.copy(ty, u, like(), like(), to).wait_send()
+                    self.copy(ty, t, like(), like(), to).wait_send()
                 if cond is None:
                     go()
                 else:
@@ -194,14 +198,18 @@
     side = lambda: (z == 0) | (z == 3)
 
     def mode(base, t):
-        if base == OA:
+        if base != OC:
             return 0
-        return t % 2 if isinstance(t, int) else lax.rem(t, 2)
+        return t % 7 % 2 if isinstance(t, int) else lax.rem(lax.rem(t + 14, 7), 2)
 
     def owner(base):
         return lambda t: z == 3 * d + mode(base, t) * (1 - 2 * d)
 
     def if_(t, cond, *acts):
+        for act in acts:
+            if hasattr(act, "before"):
+                act.before()
+
         @pl.when(cond(t))
         def _():
             for act in acts:
@@ -217,11 +225,17 @@
     def got(*a):
         return lambda: net.got(*a)
 
+    def sender(fn, base, kind, t, first, n, to, cond, **k):
+        def act():
+            fn(base, kind, t, first, n, to, cond, **k)
+        act.before = lambda: net.wait_old(base + kind, t, lambda: net.mine(base, 0, 0, n), to, cond)
+        return act
+
     def pass_on(*a):
-        return lambda: net.pass_on(*a)
+        return sender(net.pass_on, *a)
 
     def spread(*a, **k):
-        return lambda: net.spread(*a, **k)
+        return sender(net.spread, *a, **k)
 
     def z_reduce(base, k0, first_u, first_d, n):
         def climb(t):
@@ -236,7 +250,7 @@
 
         stage(k0 + z, climb)
         stage(k0 + 3 - z, sink)
-        if base != OA:
+        if base == OC:
             f = jnp.where(z >= 2, first_u, first_d)
             give = lambda t: side() & (mode(base, t) == 1)
             stage(k0, lambda t: if_(t, give, pass_on(base, W, t, f, n, cross, give)))
@@ -263,7 +277,7 @@
 
         stage(k0 + 3 - z, sink)
         stage(k0 + z, climb)
-        if not own:
+        if base == OC:
             f = jnp.where(z >= 2, first_u, first_d)
             give = lambda t: ~side() & (mode(base, t) == 1)
             stage(k0 + 1, lambda t: if_(t, give, spread(base, GW, t, f, n, cross, give)))

time: 533 us -> 527 us (0.989)
  Pallas kernels: 530 us -> 524 us
    pallas_call x1, Pallas kernels: 399 us -> 393 us  [exchange(): pl.pallas_call(functools.partial(exchange_kernel, scale), out_shape=[jax....]
where the time goes in v3:
time: 527 us; the launch traced here: 526 us
  Pallas kernels  524 us (99%)
    pallas_call x1, Pallas kernels, exchange(): pl.pallas_call(functools.partial(exchange_kernel, scale), out_shape=[jax....  393 us
    pallas_call x1, Pallas kernels, update(): pl.pallas_call(functools.partial(update_kernel, rate), in_specs=[vm] + [h...  130 us

profile of v3, /device:TPU:0, one launch (start us, length us, event | category | flops | bytes accessed | tf_op | source)
XLA Modules:
  0.0 526.5 jit_solution(5363048413154442534)
XLA Ops:
  0.6 393.4 %exchange.1 = (bf16[2,32,3072,128]{3,2,1,0:T(8,128)(2,1)}, f32[12,512,2048]{2,1,0:T(8,128)}, f32[12,2048,512]{2,1,0:T(8,128)}) custom-call(bf16[512,512]{1,0:T(8,128)(2,1)} %x_ref.2, bf16[512,512]{1,0:T(8,128)(2,1)} %y_ref.1, f32[12,512,2048]{2,1,0:T(8,128)} %w1_ref.3, f32[12,2048,512]{2,1,0:T(8,128)} %w2_ref.3, f32[12,512,2048]{2,1,0:T(8,128)} %m1_ref.1, ...), custom_call_target="tpu_custom_call" | custom-call | tf_op jit(solution)/shard_map/exchange/pallas_call | solution.py:479
  394.0 0.0 copy-start
  394.0 130.4 %update.1 = (f32[12,512,2048]{2,1,0:T(8,128)}, f32[12,2048,512]{2,1,0:T(8,128)}, f32[12,512,2048]{2,1,0:T(8,128)}, f32[12,2048,512]{2,1,0:T(8,128)}, f32[512,512]{1,0:T(8,128)}) custom-call(bf16[512,512]{1,0:T(8,128)(2,1)} %x_ref.3, f32[12,512,2048]{2,1,0:T(8,128)} %w1_ref.3, f32[12,2048,512]{2,1,0:T(8,128)} %w2_ref.3, ...), custom_call_target="tpu_custom_call" | custom-call | flops 25769803776 | bytes 402653184 | tf_op jit(solution)/shard_map/update/pallas_call | solution.py:557
  524.5 0.0 copy-done
  524.5 1.4 multiply_reduce_fusion
  525.9 0.6 broadcast_multiply_fusion
Async XLA Ops:
  394.0 130.5 %copy-start = (bf16[512,512]{1,0:T(8,128)(2,1)S(1)}, bf16[512,512]{1,0:T(8,128)(2,1)}, u32[]{:S(2)}) copy-start(bf16[512,512]{1,0:T(8,128)(2,1)} %param.15) | copy-start | bytes 1572868
